TPU v7x, 32 devices: a whole 2x2x4 slice. The times are simulated.
32 devices in a mesh: gx: 4 (over x, core), gy: 8 (over z, y).
Axes of the slice: x: 2, y: 2, z: 4, core: 2. Of those that a mesh axis runs over, the one named last changes fastest.
Arguments:
- state: float32 [512, 512, 128], P('gx', 'gy'), may hold values from -6 to 6
- diffusion: float32 [512, 512, 128], P('gx', 'gy'), may hold values from 0.01 to 0.12
- vert_inverse: float32 [512, 128, 128], P('gy'), as said below
- profiles: bfloat16 [8192, 128], P(('gx', 'gy')), may hold values from -6 to 6
- counts: int32 [32, 32], P(('gx', 'gy')), may hold values from 0 to 16, as said below
- cell_lon: int32 [8192], P(('gx', 'gy')), may hold values from 0 to 127
- cell_lat: int32 [8192], P(('gx', 'gy')), may hold values from 0 to 63
- weight_slot: int32 [2, 8192], P(None, ('gx', 'gy')), may hold values from 0 to 63
Outputs:
- adjoint: float32 [512, 512, 128], P('gx', 'gy')
Inputs may be any that keep to these rules, and one draw needn't show every extreme that they name: Each row s sums to 256; source device s stores its profiles in order of subdomain, counts[s,d] of them for subdomain d, which covers longitude cells (d // 8) * 128 onwards and latitude cells (d % 8) * 64 onwards. Some subdomain receives 16 profiles from every source. `vert_inverse`: one matrix for each latitude row.
All inputs are finite; a program needn't handle non-finite values.
Results may differ from a plain program's by a relative error of at most 0.0015.
Values may be sent and summed in bfloat16 or wider, within the bound.
A program may use at most 128 MiB of HBM per device.

v0:
```python
import functools

import jax
import jax.numpy as jnp
from jax import lax
from jax.experimental import pallas as pl
from jax.experimental.pallas import tpu as pltpu
from jax.sharding import PartitionSpec as P

CAP = 16
STEPS = 4
SLOTS = 64
PAD = 8
ROWS = 8
FIELDS = 4
F32 = jnp.float32
BF16 = jnp.bfloat16
MESH = pl.DeviceIdType.MESH
VMEM_LIMIT = 60 * 1024 * 1024


def split(value):
    upper = value.astype(BF16)
    return upper, (value - upper.astype(F32)).astype(BF16)


def iota(shape, axis):
    return lax.broadcasted_iota(jnp.int32, shape, axis)


def kernel(
    n_gx, n_gy,
    prof_ref, counts_ref, lon_ref, lat_ref, slot_ref, state_hbm, diff_hbm, inv_hbm, out_hbm,
    st, df, wf, wst, fb, obuf, msg, mmsg, recv, mrecv, wx, upper, lower,
    col_send, col_recv, row_send, row_recv, corner_send, corner_recv,
    xs, xr, ys, yr,
    w_sem, st_sem, df_sem, out_sem, v_send, v_recv, m_send, m_recv,
    f_send, f_recv, x_send, x_recv, y_send, y_recv,
):
    lon, lat, levels = state_hbm.shape
    n_all = n_gx * n_gy
    slots = n_all * CAP
    obs = prof_ref.shape[0]
    blocks = lat // ROWS
    wide = lon + 2 * PAD
    gx, gy = lax.axis_index("gx"), lax.axis_index("gy")
    me = gx * n_gy + gy
    gx_up, gx_down = lax.rem(gx + 1, n_gx), lax.rem(gx + n_gx - 1, n_gx)
    gy_up, gy_down = lax.rem(gy + 1, n_gy), lax.rem(gy + n_gy - 1, n_gy)
    east, west, north, south = (gx_up, gy), (gx_down, gy), (gx, gy_up), (gx, gy_down)

    def peer(k):
        offset = jnp.where(k % 2 == 1, (k + 1) // 2, n_all - k // 2)
        other = lax.rem(me + offset, n_all)
        return other, (other // n_gy, lax.rem(other, n_gy))

    barrier = pltpu.get_barrier_semaphore()

    def greet(k, carry):
        pl.semaphore_signal(barrier, inc=1, device_id=peer(k)[1], device_id_type=MESH)
        return carry

    lax.fori_loop(1, n_all, greet, 0)

    def block_rows(b, pitch=lon):
        return pl.ds(b * ROWS * pitch, ROWS * pitch)

    w_loads = [
        pltpu.make_async_copy(
            inv_hbm.at[pl.ds(b * ROWS, ROWS)], wf.at[pl.ds(b * ROWS, ROWS)], w_sem.at[b]
        )
        for b in range(blocks)
    ]
    for load in w_loads:
        load.start()
    for y in range(lat):
        rows = pl.ds(y * lon, lon)
        pltpu.make_async_copy(state_hbm.at[:, y, :], st.at[rows], st_sem.at[y]).start()
    for y in range(lat):
        rows = pl.ds(y * lon, lon)
        pltpu.make_async_copy(diff_hbm.at[:, y, :], df.at[rows], df_sem.at[y]).start()

    count_row = counts_ref[...].astype(F32)
    dest, lane = iota((n_all, n_all), 0), iota((n_all, n_all), 1)
    start = jnp.sum(jnp.where(lane < dest, count_row, 0.0), axis=1, keepdims=True)
    count = jnp.sum(jnp.where(lane == dest, count_row, 0.0), axis=1, keepdims=True)
    position = iota((n_all, obs), 1).astype(F32)
    inside = jnp.where((position >= start) & (position < start + count), 1.0, 0.0)
    owner = iota((n_all, obs), 0).astype(F32)
    slot_of = jnp.sum(inside * (position - start), axis=0, keepdims=True)
    code = jnp.sum(inside * owner, axis=0, keepdims=True) * CAP + slot_of
    selector = jnp.where(iota((slots, obs), 0) == code.astype(jnp.int32), 1.0, 0.0).astype(BF16)
    msg[...] = (
        jnp.dot(selector, prof_ref[...], preferred_element_type=F32)
        .astype(BF16)
        .reshape(n_all, CAP, levels)
    )
    field = iota((levels, obs), 0)
    meta = jnp.where(field < CAP, lon_ref[...].astype(F32), lat_ref[...].astype(F32))
    meta = jnp.where(field < 2 * CAP, meta, slot_ref[0:1, :].astype(F32))
    meta = jnp.where(field < 3 * CAP, meta, slot_ref[1:2, :].astype(F32))
    meta = jnp.where(field % CAP == slot_of.astype(jnp.int32), meta, 0.0).astype(BF16)
    mmsg[...] = lax.dot_general(
        inside.astype(BF16), meta, (((1,), (1,)), ((), ())), preferred_element_type=F32
    ).reshape(n_all, 1, levels)

    pl.semaphore_wait(barrier, n_all - 1)

    def block_copies(k):
        other, device = peer(k)
        return (
            pltpu.make_async_remote_copy(
                src_ref=msg.at[other], dst_ref=recv.at[k],
                send_sem=v_send.at[k], recv_sem=v_recv.at[k],
                device_id=device, device_id_type=MESH,
            ),
            pltpu.make_async_remote_copy(
                src_ref=mmsg.at[other], dst_ref=mrecv.at[k],
                send_sem=m_send.at[k], recv_sem=m_recv.at[k],
                device_id=device, device_id_type=MESH,
            ),
        )

    def send(k, carry):
        for copy in block_copies(k):
            copy.start()
        return carry

    lax.fori_loop(1, n_all, send, 0)
    recv[0] = msg[me]
    mrecv[0] = mmsg[me]

    for b in range(blocks):
        w_loads[b].wait()

        def pairs(i, carry):
            for j in range(2):
                y = b * ROWS + 2 * i + j
                wst[y] = jnp.concatenate(split(wf[y]), axis=1)
            return carry

        lax.fori_loop(0, ROWS // 2, pairs, 0)

    for y in range(lat):
        rows = pl.ds(y * lon, lon)
        pltpu.make_async_copy(state_hbm.at[:, y, :], st.at[rows], st_sem.at[y]).wait()
    st[lat * lon :, :] = jnp.zeros((lon, levels), F32)

    def arrive(k, carry):
        for copy in block_copies(k):
            copy.wait_recv()
        return carry

    lax.fori_loop(1, n_all, arrive, 0)

    table = mrecv[...].reshape(n_all, levels)
    spread = jnp.where(iota((n_all, slots), 1) // CAP == iota((n_all, slots), 0), 1.0, 0.0)
    wide_table = lax.dot_general(
        table.astype(BF16), spread.astype(BF16), (((0,), (0,)), ((), ())),
        preferred_element_type=F32,
    )
    own = iota((levels, slots), 0) % CAP == iota((levels, slots), 1) % CAP
    wide_table = jnp.where(own, wide_table, 0.0)
    lon_row, lat_row, frac_row = [
        jnp.sum(wide_table[f * CAP : (f + 1) * CAP], axis=0, keepdims=True) for f in range(3)
    ]
    frac_row = frac_row / SLOTS
    x_ids = iota((lon, slots), 0).astype(F32)
    wx_f = jnp.where(x_ids == lon_row, 1.0 - frac_row, 0.0) + jnp.where(
        x_ids == lon_row + 1.0, frac_row, 0.0
    )
    wx[...] = wx_f.astype(BF16)
    pick = iota((CAP, levels), 1) - 3 * CAP == iota((CAP, levels), 0)

    for k in range(n_all):
        here = slice(k * CAP, (k + 1) * CAP)
        frac_y = (
            jnp.sum(jnp.where(pick, mrecv[k], 0.0), axis=1, keepdims=True) / SLOTS
        )
        values = recv[k].astype(F32)
        far = values * frac_y
        near_terms, far_terms = split(values - far), split(far)
        upper[here, 0:levels], lower[here, 0:levels] = near_terms
        upper[here, levels:], lower[here, levels:] = far_terms

    def weighted(rows):
        return jnp.dot(rows, upper[...], preferred_element_type=F32) + jnp.dot(
            rows, lower[...], preferred_element_type=F32
        )

    last = jnp.where(lon_row == lon - 1.0, frac_row, 0.0)
    y_ids = iota((lat, slots), 0).astype(F32)
    edges = weighted(
        jnp.concatenate(
            [
                jnp.where(y_ids == lat_row, last, 0.0).astype(BF16),
                jnp.where(lat_row == lat - 1.0, wx_f, 0.0).astype(BF16),
            ],
            axis=0,
        )
    )
    far_col = edges[0:lat, levels:]
    shifted = jnp.where(iota((lat, levels), 0) == 0, 0.0, pltpu.roll(far_col, 1, 0))
    col_send[...] = edges[0:lat, 0:levels] + shifted
    corner_send[...] = pltpu.roll(far_col, 1, 0)[0:PAD]
    row_send[...] = edges[lat:, levels:].astype(BF16)
    f_copies = [
        pltpu.make_async_remote_copy(
            src_ref=src, dst_ref=dst, send_sem=f_send.at[i], recv_sem=f_recv.at[i],
            device_id=device, device_id_type=MESH,
        )
        for i, (src, dst, device) in enumerate(
            (
                (col_send, col_recv, east),
                (row_send, row_recv, north),
                (corner_send, corner_recv, (gx_up, gy_up)),
            )
        )
    ]
    for copy in f_copies:
        copy.start()

    group = 4

    def force(i, carry):
        parts = []
        for j in range(group):
            hot = jnp.where(lat_row == (i * group + j).astype(F32), 1.0, 0.0).astype(BF16)
            parts.append(wx[...] * hot)
        total = weighted(jnp.concatenate(parts, axis=0))
        for j in range(group + 1):
            rows = pl.ds((i * group + j) * lon, lon)
            add = None
            if j < group:
                add = total[j * lon : (j + 1) * lon, 0:levels]
            if j:
                behind = total[(j - 1) * lon : j * lon, levels:]
                add = behind if add is None else add + behind
            st[rows, :] = st[rows, :] + add
        return carry

    lax.fori_loop(0, lat // group, force, 0)
    for copy in f_copies:
        copy.wait()
    first_x = iota((lon, levels), 0) == 0
    st[0:lon, :] = st[0:lon, :] + jnp.where(
        gy > 0, row_recv[...].astype(F32) + jnp.where(first_x, corner_recv[0:1, :], 0.0), 0.0
    )
    edge = pl.ds(0, lat, stride=lon)
    st[edge, :] = st[edge, :] + col_recv[...]

    def row_at(parity, y):
        return (parity * (lat + 2) + y + 1) * wide + PAD

    def x_copies(step, b):
        copies = []
        for side, device in ((0, west), (1, east)):
            copies.append(
                pltpu.make_async_remote_copy(
                    src_ref=xs.at[step % 2, side, pl.ds(b * ROWS, ROWS)],
                    dst_ref=xr.at[step, 1 - side, pl.ds(b * ROWS, ROWS)],
                    send_sem=x_send.at[step, side, b], recv_sem=x_recv.at[step, 1 - side, b],
                    device_id=device, device_id_type=MESH,
                )
            )
        return copies

    def y_copies(step):
        return [
            pltpu.make_async_remote_copy(
                src_ref=ys.at[step % 2, side], dst_ref=yr.at[step, 1 - side],
                send_sem=y_send.at[step, side], recv_sem=y_recv.at[step, 1 - side],
                device_id=device, device_id_type=MESH,
            )
            for side, device in ((0, south), (1, north))
        ]

    def edges_in(step, b):
        for copy in x_copies(step, b):
            copy.wait()
        base = row_at(step % 2, b * ROWS)
        fb[pl.ds(base - 1, ROWS, stride=wide), :] = xr[step, 0, pl.ds(b * ROWS, ROWS), :]
        fb[pl.ds(base + lon, ROWS, stride=wide), :] = xr[step, 1, pl.ds(b * ROWS, ROWS), :]

    def advanced(step, y):
        base = row_at(step % 2, y)
        total = fb[pl.ds(base - 1, lon), :] + fb[pl.ds(base + 1, lon), :]
        total = total + (fb[pl.ds(base - wide, lon), :] + fb[pl.ds(base + wide, lon), :])
        return st[pl.ds(y * lon, lon), :] + total

    def halo(step):
        for copy in y_copies(step):
            copy.wait()
        parity = step % 2
        fb[pl.ds(row_at(parity, -1), lon), :] = jnp.where(gy > 0, yr[step, 0].astype(F32), 0.0)
        fb[pl.ds(row_at(parity, lat), lon), :] = jnp.where(
            gy < n_gy - 1, yr[step, 1].astype(F32), 0.0
        )

    def order(i):
        return jnp.where(i == 0, 0, jnp.where(i == 1, blocks - 1, i - 1))

    def section(step, y):
        rows = pl.ds(y * lon, lon)
        lam = st[rows, :] if step == 0 else advanced(step - 1, y)
        pair = wst[y]
        product = jnp.dot(
            jnp.concatenate(split(lam), axis=1),
            jnp.concatenate([pair, pair], axis=0),
            preferred_element_type=F32,
        )
        mixed = product[:, 0:levels] + product[:, levels:]
        flux = df[rows, :] * mixed
        st[rows, :] = mixed - 4.0 * flux
        fb[pl.ds(row_at(step % 2, y), lon), :] = flux

    def block(step, i, carry):
        b = order(i)
        if step:
            edges_in(step - 1, b)
        for j in range(ROWS):
            section(step, b * ROWS + j)
        base = row_at(step % 2, b * ROWS)
        part = pl.ds(b * ROWS, ROWS)
        xs[step % 2, 0, part, :] = fb[pl.ds(base, ROWS, stride=wide), :]
        xs[step % 2, 1, part, :] = fb[pl.ds(base + lon - 1, ROWS, stride=wide), :]
        for copy in x_copies(step, b):
            copy.start()
        return carry

    for y in range(lat):
        rows = pl.ds(y * lon, lon)
        pltpu.make_async_copy(diff_hbm.at[:, y, :], df.at[rows], df_sem.at[y]).wait()
    for step in range(STEPS):
        if step:
            halo(step - 1)
        lax.fori_loop(0, 2, functools.partial(block, step), 0)
        ys[step % 2, 0] = fb[pl.ds(row_at(step % 2, 0), lon), :].astype(BF16)
        ys[step % 2, 1] = fb[pl.ds(row_at(step % 2, lat - 1), lon), :].astype(BF16)
        for copy in y_copies(step):
            copy.start()
        lax.fori_loop(2, blocks, functools.partial(block, step), 0)

    halo(STEPS - 1)

    def store(y):
        return pltpu.make_async_copy(
            obuf.at[pl.ds(y * lon, lon)], out_hbm.at[:, y, :], out_sem.at[y]
        )

    def finish(i, carry):
        b = order(i)
        edges_in(STEPS - 1, b)
        for j in range(ROWS):
            y = b * ROWS + j
            obuf[pl.ds(y * lon, lon), :] = advanced(STEPS - 1, y)
            store(y).start()
        return carry

    lax.fori_loop(0, blocks, finish, 0)

    def sent(k, carry):
        for copy in block_copies(k):
            copy.wait_send()
        return carry

    lax.fori_loop(1, n_all, sent, 0)

    def stored(y, carry):
        store(y).wait()
        return carry

    lax.fori_loop(0, lat, stored, 0)


def solution(mesh):
    n_gx, n_gy = mesh.shape["gx"], mesh.shape["gy"]

    def shards(state, diffusion, vert_inverse, profiles, counts, cell_lon, cell_lat, weight_slot):
        lon, lat, levels = state.shape
        n_all = counts.shape[1]
        slots = n_all * CAP
        blocks = lat // ROWS
        wide = lon + 2 * PAD
        dma = pltpu.SemaphoreType.DMA
        vmem = pl.BlockSpec(memory_space=pltpu.VMEM)
        out = pl.pallas_call(
            functools.partial(kernel, n_gx, n_gy),
            out_shape=jax.ShapeDtypeStruct((lon, lat, levels), F32),
            in_specs=[vmem] * 5 + [pl.BlockSpec(memory_space=pl.ANY)] * 3,
            out_specs=pl.BlockSpec(memory_space=pl.ANY),
            scratch_shapes=[
                pltpu.VMEM(((lat + 1) * lon, levels), F32),
                pltpu.VMEM((lat * lon, levels), F32),
                pltpu.VMEM((lat, levels, levels), F32),
                pltpu.VMEM((lat, levels, 2 * levels), BF16),
                pltpu.VMEM((2 * (lat + 2) * wide, levels), F32),
                pltpu.VMEM((lat * lon, levels), F32),
                pltpu.VMEM((n_all, CAP, levels), BF16),
                pltpu.VMEM((n_all, 1, levels), F32),
                pltpu.VMEM((n_all, CAP, levels), BF16),
                pltpu.VMEM((n_all, 1, levels), F32),
                pltpu.VMEM((lon, slots), BF16),
                pltpu.VMEM((slots, 2 * levels), BF16),
                pltpu.VMEM((slots, 2 * levels), BF16),
                pltpu.VMEM((lat, levels), F32),
                pltpu.VMEM((lat, levels), F32),
                pltpu.VMEM((lon, levels), BF16),
                pltpu.VMEM((lon, levels), BF16),
                pltpu.VMEM((PAD, levels), F32),
                pltpu.VMEM((PAD, levels), F32),
                pltpu.VMEM((2, 2, lat, levels), F32),
                pltpu.VMEM((STEPS, 2, lat, levels), F32),
                pltpu.VMEM((2, 2, lon, levels), BF16),
                pltpu.VMEM((STEPS, 2, lon, levels), BF16),
                dma((blocks,)), dma((lat,)), dma((lat,)), dma((lat,)),
                dma((n_all,)), dma((n_all,)), dma((n_all,)), dma((n_all,)),
                dma((3,)), dma((3,)),
                dma((STEPS, 2, blocks)), dma((STEPS, 2, blocks)),
                dma((STEPS, 2)), dma((STEPS, 2)),
            ],
            compiler_params=pltpu.CompilerParams(
                collective_id=0, has_side_effects=True, vmem_limit_bytes=VMEM_LIMIT
            ),
            name="adjoint",
        )(
            profiles, counts, cell_lon[None], cell_lat[None], weight_slot,
            state, diffusion, vert_inverse,
        )
        return out

    return jax.shard_map(
        shards,
        mesh=mesh,
        in_specs=(
            P("gx", "gy", None),
            P("gx", "gy", None),
            P("gy", None, None),
            P(("gx", "gy"), None),
            P(("gx", "gy"), None),
            P(("gx", "gy")),
            P(("gx", "gy")),
            P(None, ("gx", "gy")),
        ),
        out_specs=P("gx", "gy", None),
        check_vma=False,
    )
```

profile of v0, /device:TPU:0, one launch (start us, length us, event | category | flops | bytes accessed | tf_op | source)
XLA Modules:
  0.0 51.3 jit_solution(15313769477208053496)
XLA Ops:
  0.0 46.5 %adjoint.1 = f32[128,64,128]{2,1,0:T(8,128)} custom-call(bf16[256,128]{1,0:T(8,128)(2,1)} %prof_ref.1, s32[1,32]{1,0:T(1,128)} %counts_ref.1, s32[1,256]{1,0:T(1,128)} %bitcast.2, s32[1,256]{1,0:T(1,128)} %bitcast.3, s32[2,256]{1,0:T(2,128)} %slot_ref.1, f32[128,64,128]{2,1,0:T(8,128)} %state_hbm.1, f32[128,64,128]{2,1,0:T(8,128)} %diff_hbm.1, ...), custom_call_target="tpu_custom_call" | custom-call | tf_op jit(solution)/shard_map/adjoint/pallas_call | solution.py:387
  46.6 4.8 %copy.10 = f32[128,64,128]{2,1,0:T(8,128)} copy(f32[128,64,128]{2,1,0:T(8,128)} %adjoint.1) | data formatting | bytes 8388608
where the time goes:
time: 52 us; the launch traced here: 51.3 us
  Pallas kernels  46.5 us (89%)
  local copies, waits for them, and re-layouts  4.79 us (9%)
    pallas_call x1, Pallas kernels, shards(): pl.pallas_call(functools.partial(kernel, n_gx, n_gy), out_shape=jax.Shape...  46.5 us
    unnamed x1, local copies, waits for them, and re-layouts  4.79 us

commit v1 on v0

--- a/solution.py
+++ b/solution.py
@@ -12,11 +12,12 @@
 SLOTS = 64
 PAD = 8
 ROWS = 8
+HALF = ROWS // 2
 FIELDS = 4
 F32 = jnp.float32
 BF16 = jnp.bfloat16
 MESH = pl.DeviceIdType.MESH
-VMEM_LIMIT = 60 * 1024 * 1024
+VMEM_LIMIT = 48 * 1024 * 1024
 
 
 def split(value):
@@ -30,11 +31,11 @@
 
 def kernel(
     n_gx, n_gy,
-    prof_ref, counts_ref, lon_ref, lat_ref, slot_ref, state_hbm, diff_hbm, inv_hbm, out_hbm,
-    st, df, wf, wst, fb, obuf, msg, mmsg, recv, mrecv, wx, upper, lower,
-    col_send, col_recv, row_send, row_recv, corner_send, corner_recv,
+    prof_hbm, counts_hbm, lon_hbm, lat_hbm, slot_hbm, state_hbm, diff_hbm, inv_hbm, obuf,
+    prof_ref, counts_ref, lon_ref, lat_ref, slot_ref, st, df, wf, wst, fb, msg, mmsg, recv, mrecv, wx, upper, lower,
+    col_send, col_recv, near_row, row_send, row_recv, corner_send, corner_recv,
     xs, xr, ys, yr,
-    w_sem, st_sem, df_sem, out_sem, v_send, v_recv, m_send, m_recv,
+    small_sem, w_sem, st_sem, df_sem, v_send, v_recv, m_send, m_recv,
     f_send, f_recv, x_send, x_recv, y_send, y_recv,
 ):
     lon, lat, levels = state_hbm.shape
@@ -49,21 +50,25 @@
     gy_up, gy_down = lax.rem(gy + 1, n_gy), lax.rem(gy + n_gy - 1, n_gy)
     east, west, north, south = (gx_up, gy), (gx_down, gy), (gx, gy_up), (gx, gy_down)
 
-    def peer(k):
-        offset = jnp.where(k % 2 == 1, (k + 1) // 2, n_all - k // 2)
-        other = lax.rem(me + offset, n_all)
-        return other, (other // n_gy, lax.rem(other, n_gy))
+    small_loads = [
+        pltpu.make_async_copy(src, dst, small_sem.at[i])
+        for i, (src, dst) in enumerate(
+            (
+                (counts_hbm, counts_ref), (prof_hbm, prof_ref), (lon_hbm, lon_ref),
+                (lat_hbm, lat_ref), (slot_hbm, slot_ref),
+            )
+        )
+    ]
+    for load in small_loads:
+        load.start()
+
+    columns = [lax.rem(gx + d, n_gx) for d in range(n_gx)]
+    lines = [lax.rem(gy + d, n_gy) for d in range(n_gy)]
+    peers = [(column, line) for column in columns for line in lines]
 
     barrier = pltpu.get_barrier_semaphore()
-
-    def greet(k, carry):
-        pl.semaphore_signal(barrier, inc=1, device_id=peer(k)[1], device_id_type=MESH)
-        return carry
-
-    lax.fori_loop(1, n_all, greet, 0)
-
-    def block_rows(b, pitch=lon):
-        return pl.ds(b * ROWS * pitch, ROWS * pitch)
+    for peer in peers[1:]:
+        pl.semaphore_signal(barrier, inc=1, device_id=peer, device_id_type=MESH)
 
     w_loads = [
         pltpu.make_async_copy(
@@ -79,6 +84,9 @@
     for y in range(lat):
         rows = pl.ds(y * lon, lon)
         pltpu.make_async_copy(diff_hbm.at[:, y, :], df.at[rows], df_sem.at[y]).start()
+
+    for load in small_loads:
+        load.wait()
 
     count_row = counts_ref[...].astype(F32)
     dest, lane = iota((n_all, n_all), 0), iota((n_all, n_all), 1)
@@ -106,27 +114,21 @@
 
     pl.semaphore_wait(barrier, n_all - 1)
 
-    def block_copies(k):
-        other, device = peer(k)
-        return (
-            pltpu.make_async_remote_copy(
-                src_ref=msg.at[other], dst_ref=recv.at[k],
-                send_sem=v_send.at[k], recv_sem=v_recv.at[k],
-                device_id=device, device_id_type=MESH,
-            ),
-            pltpu.make_async_remote_copy(
-                src_ref=mmsg.at[other], dst_ref=mrecv.at[k],
-                send_sem=m_send.at[k], recv_sem=m_recv.at[k],
-                device_id=device, device_id_type=MESH,
-            ),
-        )
-
-    def send(k, carry):
-        for copy in block_copies(k):
-            copy.start()
-        return carry
-
-    lax.fori_loop(1, n_all, send, 0)
+    sends = []
+    for k, (column, line) in enumerate(peers[1:], 1):
+        other = column * n_gy + line
+        for src, dst, send_sem, recv_sem in (
+            (msg, recv, v_send, v_recv), (mmsg, mrecv, m_send, m_recv)
+        ):
+            sends.append(
+                pltpu.make_async_remote_copy(
+                    src_ref=src.at[other], dst_ref=dst.at[k],
+                    send_sem=send_sem.at[k], recv_sem=recv_sem.at[k],
+                    device_id=(column, line), device_id_type=MESH,
+                )
+            )
+    for copy in sends:
+        copy.start()
     recv[0] = msg[me]
     mrecv[0] = mmsg[me]
 
@@ -144,14 +146,9 @@
     for y in range(lat):
         rows = pl.ds(y * lon, lon)
         pltpu.make_async_copy(state_hbm.at[:, y, :], st.at[rows], st_sem.at[y]).wait()
-    st[lat * lon :, :] = jnp.zeros((lon, levels), F32)
-
-    def arrive(k, carry):
-        for copy in block_copies(k):
-            copy.wait_recv()
-        return carry
-
-    lax.fori_loop(1, n_all, arrive, 0)
+
+    for copy in sends:
+        copy.wait_recv()
 
     table = mrecv[...].reshape(n_all, levels)
     spread = jnp.where(iota((n_all, slots), 1) // CAP == iota((n_all, slots), 0), 1.0, 0.0)
@@ -204,6 +201,7 @@
     col_send[...] = edges[0:lat, 0:levels] + shifted
     corner_send[...] = pltpu.roll(far_col, 1, 0)[0:PAD]
     row_send[...] = edges[lat:, levels:].astype(BF16)
+    near_row[...] = edges[lat:, 0:levels]
     f_copies = [
         pltpu.make_async_remote_copy(
             src_ref=src, dst_ref=dst, send_sem=f_send.at[i], recv_sem=f_recv.at[i],
@@ -220,26 +218,40 @@
     for copy in f_copies:
         copy.start()
 
-    group = 4
-
-    def force(i, carry):
+    done_row = lat - HALF - 1
+
+    def force(runs, edge):
         parts = []
-        for j in range(group):
-            hot = jnp.where(lat_row == (i * group + j).astype(F32), 1.0, 0.0).astype(BF16)
-            parts.append(wx[...] * hot)
+        for low, size in runs:
+            for j in range(size):
+                y = low + j
+                if not edge:
+                    y = jnp.where(y == done_row, -1, y).astype(F32)
+                hot = jnp.where(lat_row == y, 1.0, 0.0).astype(BF16)
+                parts.append(wx[...] * hot)
         total = weighted(jnp.concatenate(parts, axis=0))
-        for j in range(group + 1):
-            rows = pl.ds((i * group + j) * lon, lon)
-            add = None
-            if j < group:
-                add = total[j * lon : (j + 1) * lon, 0:levels]
-            if j:
-                behind = total[(j - 1) * lon : j * lon, levels:]
-                add = behind if add is None else add + behind
-            st[rows, :] = st[rows, :] + add
+        at = 0
+        for low, size in runs:
+            for j in range(size + 1):
+                rows = pl.ds((low + j) * lon, lon)
+                add = None
+                if j < size:
+                    add = total[at * lon : (at + 1) * lon, 0:levels]
+                if j:
+                    behind = total[(at - 1) * lon : at * lon, levels:]
+                    add = behind if add is None else add + behind
+                st[rows, :] = st[rows, :] + add
+                at = at + 1 if j < size else at
+
+    def force_block(b, carry):
+        force([(HALF + (b - 1) * ROWS, ROWS)], False)
         return carry
 
-    lax.fori_loop(0, lat // group, force, 0)
+    force([(0, HALF), (done_row, HALF)], True)
+    final = pl.ds((lat - 1) * lon, lon)
+    st[final, :] = st[final, :] + near_row[...]
+    early = blocks // 2 + 1
+    lax.fori_loop(1, early, force_block, 0)
     for copy in f_copies:
         copy.wait()
     first_x = iota((lon, levels), 0) == 0
@@ -275,12 +287,19 @@
             for side, device in ((0, south), (1, north))
         ]
 
-    def edges_in(step, b):
+    def segments(b, edge):
+        if edge:
+            return [(0, HALF, 0), (lat - HALF, HALF, HALF)]
+        return [(HALF + (b - 1) * ROWS, ROWS, b * ROWS)]
+
+    def edges_in(step, b, edge):
         for copy in x_copies(step, b):
             copy.wait()
-        base = row_at(step % 2, b * ROWS)
-        fb[pl.ds(base - 1, ROWS, stride=wide), :] = xr[step, 0, pl.ds(b * ROWS, ROWS), :]
-        fb[pl.ds(base + lon, ROWS, stride=wide), :] = xr[step, 1, pl.ds(b * ROWS, ROWS), :]
+        for low, size, at in segments(b, edge):
+            base = row_at(step % 2, low)
+            part = pl.ds(at, size)
+            fb[pl.ds(base - 1, size, stride=wide), :] = xr[step, 0, part, :]
+            fb[pl.ds(base + lon, size, stride=wide), :] = xr[step, 1, part, :]
 
     def advanced(step, y):
         base = row_at(step % 2, y)
@@ -296,9 +315,6 @@
         fb[pl.ds(row_at(parity, lat), lon), :] = jnp.where(
             gy < n_gy - 1, yr[step, 1].astype(F32), 0.0
         )
-
-    def order(i):
-        return jnp.where(i == 0, 0, jnp.where(i == 1, blocks - 1, i - 1))
 
     def section(step, y):
         rows = pl.ds(y * lon, lon)
@@ -314,63 +330,78 @@
         st[rows, :] = mixed - 4.0 * flux
         fb[pl.ds(row_at(step % 2, y), lon), :] = flux
 
-    def block(step, i, carry):
-        b = order(i)
+    def block(step, b, edge):
         if step:
-            edges_in(step - 1, b)
-        for j in range(ROWS):
-            section(step, b * ROWS + j)
-        base = row_at(step % 2, b * ROWS)
-        part = pl.ds(b * ROWS, ROWS)
-        xs[step % 2, 0, part, :] = fb[pl.ds(base, ROWS, stride=wide), :]
-        xs[step % 2, 1, part, :] = fb[pl.ds(base + lon - 1, ROWS, stride=wide), :]
+            edges_in(step - 1, b, edge)
+        for low, size, _ in segments(b, edge):
+            for j in range(size):
+                section(step, low + j)
+        for low, size, at in segments(b, edge):
+            base = row_at(step % 2, low)
+            part = pl.ds(at, size)
+            xs[step % 2, 0, part, :] = fb[pl.ds(base, size, stride=wide), :]
+            xs[step % 2, 1, part, :] = fb[pl.ds(base + lon - 1, size, stride=wide), :]
         for copy in x_copies(step, b):
             copy.start()
-        return carry
-
-    for y in range(lat):
-        rows = pl.ds(y * lon, lon)
-        pltpu.make_async_copy(diff_hbm.at[:, y, :], df.at[rows], df_sem.at[y]).wait()
-    for step in range(STEPS):
+
+    def edge_block(step):
         if step:
             halo(step - 1)
-        lax.fori_loop(0, 2, functools.partial(block, step), 0)
+        block(step, 0, True)
         ys[step % 2, 0] = fb[pl.ds(row_at(step % 2, 0), lon), :].astype(BF16)
         ys[step % 2, 1] = fb[pl.ds(row_at(step % 2, lat - 1), lon), :].astype(BF16)
         for copy in y_copies(step):
             copy.start()
-        lax.fori_loop(2, blocks, functools.partial(block, step), 0)
-
+
+    def inner_blocks(step, low, high):
+        def one(b, carry):
+            block(step, b, False)
+            return carry
+
+        lax.fori_loop(low, high, one, 0)
+
+    def finish(b, edge):
+        edges_in(STEPS - 1, b, edge)
+        for low, size, _ in segments(b, edge):
+            for j in range(size):
+                obuf[pl.ds((low + j) * lon, lon), :] = advanced(STEPS - 1, low + j)
+
+    def finish_inner(b, carry):
+        finish(b, False)
+        return carry
+
+    for y in range(lat):
+        rows = pl.ds(y * lon, lon)
+        pltpu.make_async_copy(diff_hbm.at[:, y, :], df.at[rows], df_sem.at[y]).wait()
+    edge_block(0)
+    lax.fori_loop(early, blocks, force_block, 0)
+    inner_blocks(0, 1, blocks)
+    edge_block(1)
+    inner_blocks(1, 1, blocks)
+    inner_blocks(2, 1, early)
+    edge_block(2)
+    inner_blocks(2, early, blocks)
+    inner_blocks(3, 1, blocks)
+    edge_block(3)
+    lax.fori_loop(1, blocks, finish_inner, 0)
     halo(STEPS - 1)
+    finish(0, True)
+    for copy in sends:
+        copy.wait_send()
+
+
+def store_kernel(rows_ref, out_hbm, sem):
+    lon, lat, _ = out_hbm.shape
 
     def store(y):
         return pltpu.make_async_copy(
-            obuf.at[pl.ds(y * lon, lon)], out_hbm.at[:, y, :], out_sem.at[y]
-        )
-
-    def finish(i, carry):
-        b = order(i)
-        edges_in(STEPS - 1, b)
-        for j in range(ROWS):
-            y = b * ROWS + j
-            obuf[pl.ds(y * lon, lon), :] = advanced(STEPS - 1, y)
-            store(y).start()
-        return carry
-
-    lax.fori_loop(0, blocks, finish, 0)
-
-    def sent(k, carry):
-        for copy in block_copies(k):
-            copy.wait_send()
-        return carry
-
-    lax.fori_loop(1, n_all, sent, 0)
-
-    def stored(y, carry):
+            rows_ref.at[pl.ds(y * lon, lon)], out_hbm.at[:, y, :], sem.at[y]
+        )
+
+    for y in range(lat):
+        store(y).start()
+    for y in range(lat):
         store(y).wait()
-        return carry
-
-    lax.fori_loop(0, lat, stored, 0)
 
 
 def solution(mesh):
@@ -384,18 +415,23 @@
         wide = lon + 2 * PAD
         dma = pltpu.SemaphoreType.DMA
         vmem = pl.BlockSpec(memory_space=pltpu.VMEM)
+        obs = profiles.shape[0]
         out = pl.pallas_call(
             functools.partial(kernel, n_gx, n_gy),
-            out_shape=jax.ShapeDtypeStruct((lon, lat, levels), F32),
-            in_specs=[vmem] * 5 + [pl.BlockSpec(memory_space=pl.ANY)] * 3,
-            out_specs=pl.BlockSpec(memory_space=pl.ANY),
+            out_shape=pltpu.VMEM((lat * lon, levels), F32),
+            in_specs=[pl.BlockSpec(memory_space=pltpu.HBM)] * 8,
+            out_specs=vmem,
             scratch_shapes=[
-                pltpu.VMEM(((lat + 1) * lon, levels), F32),
+                pltpu.VMEM((obs, levels), BF16),
+                pltpu.VMEM((1, n_all), jnp.int32),
+                pltpu.VMEM((1, obs), jnp.int32),
+                pltpu.VMEM((1, obs), jnp.int32),
+                pltpu.VMEM((2, obs), jnp.int32),
+                pltpu.VMEM((lat * lon, levels), F32),
                 pltpu.VMEM((lat * lon, levels), F32),
                 pltpu.VMEM((lat, levels, levels), F32),
                 pltpu.VMEM((lat, levels, 2 * levels), BF16),
                 pltpu.VMEM((2 * (lat + 2) * wide, levels), F32),
-                pltpu.VMEM((lat * lon, levels), F32),
                 pltpu.VMEM((n_all, CAP, levels), BF16),
                 pltpu.VMEM((n_all, 1, levels), F32),
                 pltpu.VMEM((n_all, CAP, levels), BF16),
@@ -405,6 +441,7 @@
                 pltpu.VMEM((slots, 2 * levels), BF16),
                 pltpu.VMEM((lat, levels), F32),
                 pltpu.VMEM((lat, levels), F32),
+                pltpu.VMEM((lon, levels), F32),
                 pltpu.VMEM((lon, levels), BF16),
                 pltpu.VMEM((lon, levels), BF16),
                 pltpu.VMEM((PAD, levels), F32),
@@ -413,7 +450,7 @@
                 pltpu.VMEM((STEPS, 2, lat, levels), F32),
                 pltpu.VMEM((2, 2, lon, levels), BF16),
                 pltpu.VMEM((STEPS, 2, lon, levels), BF16),
-                dma((blocks,)), dma((lat,)), dma((lat,)), dma((lat,)),
+                dma((5,)), dma((blocks,)), dma((lat,)), dma((lat,)),
                 dma((n_all,)), dma((n_all,)), dma((n_all,)), dma((n_all,)),
                 dma((3,)), dma((3,)),
                 dma((STEPS, 2, blocks)), dma((STEPS, 2, blocks)),
@@ -424,10 +461,23 @@
             ),
             name="adjoint",
         )(
-            profiles, counts, cell_lon[None], cell_lat[None], weight_slot,
-            state, diffusion, vert_inverse,
-        )
-        return out
+            *[
+                pltpu.with_memory_space_constraint(x, pltpu.HBM)
+                for x in (
+                    profiles, counts, cell_lon[None], cell_lat[None], weight_slot,
+                    state, diffusion, vert_inverse,
+                )
+            ]
+        )
+        return pl.pallas_call(
+            store_kernel,
+            out_shape=jax.ShapeDtypeStruct((lon, lat, levels), F32),
+            in_specs=[vmem],
+            out_specs=pl.BlockSpec(memory_space=pl.ANY),
+            scratch_shapes=[dma((lat,))],
+            compiler_params=pltpu.CompilerParams(vmem_limit_bytes=8 * 1024 * 1024),
+            name="store",
+        )(pltpu.with_memory_space_constraint(out, pltpu.VMEM))
 
     return jax.shard_map(
         shards,

time: 52 us -> 43.1 us (0.83); the launches traced: 51.3 us -> 43 us
  local copies, waits for them, and re-layouts: 4.79 us -> 0 us
  Pallas kernels: 46.5 us -> 43 us
    unnamed x1 -> x0, local copies, waits for them, and re-layouts: 4.79 us -> none
    pallas_call x1 -> x2, Pallas kernels: 46.5 us -> 43 us  [the longest x1 40.5 us: shards(): pl.pallas_call(functools.partial(kernel, n_gx, n_gy), out_shape=pltpu.VME...]
where the time goes in v1:
time: 43.1 us; the launch traced here: 43 us
  Pallas kernels  43 us (100%)
    pallas_call x1, Pallas kernels, shards(): pl.pallas_call(functools.partial(kernel, n_gx, n_gy), out_shape=pltpu.VME...  40.5 us
    pallas_call x1, Pallas kernels, shards(): pl.pallas_call(store_kernel, out_shape=jax.ShapeDtypeStruct((lon, lat, le...  2.53 us

profile of v1, /device:TPU:0, one launch (start us, length us, event | category | flops | bytes accessed | tf_op | source)
XLA Modules:
  0.0 43.0 jit_solution(12739330000104769958)
XLA Ops:
  0.0 40.5 %adjoint.1.rows_ref = f32[8192,128]{1,0:T(8,128)S(1)} custom-call(bf16[256,128]{1,0:T(8,128)(2,1)} %prof_hbm.1, s32[1,32]{1,0:T(1,128)} %counts_hbm.1, s32[1,256]{1,0:T(1,128)} %bitcast.2, s32[1,256]{1,0:T(1,128)} %bitcast.3, s32[2,256]{1,0:T(2,128)} %slot_hbm.1, f32[128,64,128]{2,1,0:T(8,128)} %state_hbm.1, f32[128,64,128]{2,1,0:T(8,128)} %diff_hbm.1, ...), custom_call_target="tpu_custom_call" | custom-call | tf_op jit(solution)/shard_map/adjoint/pallas_call | solution.py:419
  40.5 2.5 %store.1 = f32[128,64,128]{2,1,0:T(8,128)} custom-call(f32[8192,128]{1,0:T(8,128)S(1)} %adjoint.1.rows_ref), custom_call_target="tpu_custom_call" | custom-call | tf_op jit(solution)/shard_map/store/pallas_call | solution.py:472

commit v2 on v1

--- a/solution.py
+++ b/solution.py
@@ -70,6 +70,9 @@
     for peer in peers[1:]:
         pl.semaphore_signal(barrier, inc=1, device_id=peer, device_id_type=MESH)
 
+    for load in small_loads:
+        load.wait()
+
     w_loads = [
         pltpu.make_async_copy(
             inv_hbm.at[pl.ds(b * ROWS, ROWS)], wf.at[pl.ds(b * ROWS, ROWS)], w_sem.at[b]
@@ -84,9 +87,6 @@
     for y in range(lat):
         rows = pl.ds(y * lon, lon)
         pltpu.make_async_copy(diff_hbm.at[:, y, :], df.at[rows], df_sem.at[y]).start()
-
-    for load in small_loads:
-        load.wait()
 
     count_row = counts_ref[...].astype(F32)
     dest, lane = iota((n_all, n_all), 0), iota((n_all, n_all), 1)
@@ -147,8 +147,25 @@
         rows = pl.ds(y * lon, lon)
         pltpu.make_async_copy(state_hbm.at[:, y, :], st.at[rows], st_sem.at[y]).wait()
 
-    for copy in sends:
-        copy.wait_recv()
+    for y in range(lat):
+        rows = pl.ds(y * lon, lon)
+        pltpu.make_async_copy(diff_hbm.at[:, y, :], df.at[rows], df_sem.at[y]).wait()
+
+    pick = iota((CAP, levels), 1) - 3 * CAP == iota((CAP, levels), 0)
+    batch = n_all
+    for k in range(n_all):
+        if k % batch == 0:
+            for copy in sends[max(2 * k - 2, 0) : 2 * (k + batch) - 2]:
+                copy.wait_recv()
+        here = slice(k * CAP, (k + 1) * CAP)
+        frac_y = (
+            jnp.sum(jnp.where(pick, mrecv[k], 0.0), axis=1, keepdims=True) / SLOTS
+        )
+        values = recv[k].astype(F32)
+        far = values * frac_y
+        near_terms, far_terms = split(values - far), split(far)
+        upper[here, 0:levels], lower[here, 0:levels] = near_terms
+        upper[here, levels:], lower[here, levels:] = far_terms
 
     table = mrecv[...].reshape(n_all, levels)
     spread = jnp.where(iota((n_all, slots), 1) // CAP == iota((n_all, slots), 0), 1.0, 0.0)
@@ -167,19 +184,6 @@
         x_ids == lon_row + 1.0, frac_row, 0.0
     )
     wx[...] = wx_f.astype(BF16)
-    pick = iota((CAP, levels), 1) - 3 * CAP == iota((CAP, levels), 0)
-
-    for k in range(n_all):
-        here = slice(k * CAP, (k + 1) * CAP)
-        frac_y = (
-            jnp.sum(jnp.where(pick, mrecv[k], 0.0), axis=1, keepdims=True) / SLOTS
-        )
-        values = recv[k].astype(F32)
-        far = values * frac_y
-        near_terms, far_terms = split(values - far), split(far)
-        upper[here, 0:levels], lower[here, 0:levels] = near_terms
-        upper[here, levels:], lower[here, levels:] = far_terms
-
     def weighted(rows):
         return jnp.dot(rows, upper[...], preferred_element_type=F32) + jnp.dot(
             rows, lower[...], preferred_element_type=F32
@@ -250,16 +254,27 @@
     force([(0, HALF), (done_row, HALF)], True)
     final = pl.ds((lat - 1) * lon, lon)
     st[final, :] = st[final, :] + near_row[...]
-    early = blocks // 2 + 1
+    early = (3 * blocks) // 4
+    middle = (3 * blocks) // 4
     lax.fori_loop(1, early, force_block, 0)
     for copy in f_copies:
         copy.wait()
     first_x = iota((lon, levels), 0) == 0
+
+    def add_column(y):
+        rows = pl.ds(y * lon, lon)
+        st[rows, :] = st[rows, :] + jnp.where(first_x, col_recv[y : y + 1, :], 0.0)
+
+    def add_columns():
+        y = iota((lat, levels), 0)
+        edge = pl.ds(0, lat, stride=lon)
+        st[edge, :] = st[edge, :] + jnp.where((y > 0) & (y < lat - 1), col_recv[...], 0.0)
+
     st[0:lon, :] = st[0:lon, :] + jnp.where(
         gy > 0, row_recv[...].astype(F32) + jnp.where(first_x, corner_recv[0:1, :], 0.0), 0.0
     )
-    edge = pl.ds(0, lat, stride=lon)
-    st[edge, :] = st[edge, :] + col_recv[...]
+    add_column(0)
+    add_column(lat - 1)
 
     def row_at(parity, y):
         return (parity * (lat + 2) + y + 1) * wide + PAD
@@ -329,13 +344,9 @@
         flux = df[rows, :] * mixed
         st[rows, :] = mixed - 4.0 * flux
         fb[pl.ds(row_at(step % 2, y), lon), :] = flux
-
-    def block(step, b, edge):
-        if step:
-            edges_in(step - 1, b, edge)
-        for low, size, _ in segments(b, edge):
-            for j in range(size):
-                section(step, low + j)
+        return flux
+
+    def share(step, b, edge):
         for low, size, at in segments(b, edge):
             base = row_at(step % 2, low)
             part = pl.ds(at, size)
@@ -346,48 +357,59 @@
 
     def edge_block(step):
         if step:
+            edges_in(step - 1, 0, True)
             halo(step - 1)
-        block(step, 0, True)
-        ys[step % 2, 0] = fb[pl.ds(row_at(step % 2, 0), lon), :].astype(BF16)
-        ys[step % 2, 1] = fb[pl.ds(row_at(step % 2, lat - 1), lon), :].astype(BF16)
+        for side, y in enumerate((0, lat - 1)):
+            ys[step % 2, side] = section(step, y).astype(BF16)
         for copy in y_copies(step):
             copy.start()
+        if step == 0:
+            add_columns()
+        for j in range(1, HALF):
+            section(step, j)
+            section(step, lat - 1 - j)
+        share(step, 0, True)
 
     def inner_blocks(step, low, high):
         def one(b, carry):
-            block(step, b, False)
+            if step:
+                edges_in(step - 1, b, False)
+            for j in range(ROWS):
+                section(step, HALF + (b - 1) * ROWS + j)
+            share(step, b, False)
             return carry
 
         lax.fori_loop(low, high, one, 0)
 
-    def finish(b, edge):
-        edges_in(STEPS - 1, b, edge)
-        for low, size, _ in segments(b, edge):
-            for j in range(size):
-                obuf[pl.ds((low + j) * lon, lon), :] = advanced(STEPS - 1, low + j)
+    def finish_row(y):
+        obuf[pl.ds(y * lon, lon), :] = advanced(STEPS - 1, y)
 
     def finish_inner(b, carry):
-        finish(b, False)
+        edges_in(STEPS - 1, b, False)
+        for j in range(ROWS):
+            finish_row(HALF + (b - 1) * ROWS + j)
         return carry
 
-    for y in range(lat):
-        rows = pl.ds(y * lon, lon)
-        pltpu.make_async_copy(diff_hbm.at[:, y, :], df.at[rows], df_sem.at[y]).wait()
     edge_block(0)
     lax.fori_loop(early, blocks, force_block, 0)
     inner_blocks(0, 1, blocks)
     edge_block(1)
     inner_blocks(1, 1, blocks)
-    inner_blocks(2, 1, early)
+    inner_blocks(2, 1, middle)
     edge_block(2)
-    inner_blocks(2, early, blocks)
+    inner_blocks(2, middle, blocks)
     inner_blocks(3, 1, blocks)
     edge_block(3)
     lax.fori_loop(1, blocks, finish_inner, 0)
-    halo(STEPS - 1)
-    finish(0, True)
+    edges_in(STEPS - 1, 0, True)
+    for j in range(1, HALF):
+        finish_row(j)
+        finish_row(lat - 1 - j)
     for copy in sends:
         copy.wait_send()
+    halo(STEPS - 1)
+    finish_row(0)
+    finish_row(lat - 1)
 
 
 def store_kernel(rows_ref, out_hbm, sem):

time: 43.1 us -> 42.1 us (0.977)
  Pallas kernels: 43 us -> 41.9 us
    pallas_call x1, Pallas kernels: 40.5 us -> 39.4 us  [shards(): pl.pallas_call(functools.partial(kernel, n_gx, n_gy), out_shape=pltpu.VME...]
where the time goes in v2:
time: 42.1 us; the launch traced here: 41.9 us
  Pallas kernels  41.9 us (100%)
    pallas_call x1, Pallas kernels, shards(): pl.pallas_call(functools.partial(kernel, n_gx, n_gy), out_shape=pltpu.VME...  39.4 us
    pallas_call x1, Pallas kernels, shards(): pl.pallas_call(store_kernel, out_shape=jax.ShapeDtypeStruct((lon, lat, le...  2.53 us

profile of v2, /device:TPU:0, one launch (start us, length us, event | category | flops | bytes accessed | tf_op | source)
XLA Modules:
  0.0 41.9 jit_solution(7814290937218494491)
XLA Ops:
  0.0 39.4 %adjoint.1.rows_ref = f32[8192,128]{1,0:T(8,128)S(1)} custom-call(bf16[256,128]{1,0:T(8,128)(2,1)} %prof_hbm.1, s32[1,32]{1,0:T(1,128)} %counts_hbm.1, s32[1,256]{1,0:T(1,128)} %bitcast.2, s32[1,256]{1,0:T(1,128)} %bitcast.3, s32[2,256]{1,0:T(2,128)} %slot_hbm.1, f32[128,64,128]{2,1,0:T(8,128)} %state_hbm.1, f32[128,64,128]{2,1,0:T(8,128)} %diff_hbm.1, ...), custom_call_target="tpu_custom_call" | custom-call | tf_op jit(solution)/shard_map/adjoint/pallas_call | solution.py:441
  39.4 2.5 %store.1 = f32[128,64,128]{2,1,0:T(8,128)} custom-call(f32[8192,128]{1,0:T(8,128)S(1)} %adjoint.1.rows_ref), custom_call_target="tpu_custom_call" | custom-call | tf_op jit(solution)/shard_map/store/pallas_call | solution.py:494

commit v3 on v2

--- a/solution.py
+++ b/solution.py
@@ -123,7 +123,7 @@
             sends.append(
                 pltpu.make_async_remote_copy(
                     src_ref=src.at[other], dst_ref=dst.at[k],
-                    send_sem=send_sem.at[k], recv_sem=recv_sem.at[k],
+                    send_sem=send_sem.at[0], recv_sem=recv_sem.at[0],
                     device_id=(column, line), device_id_type=MESH,
                 )
             )
@@ -152,11 +152,10 @@
         pltpu.make_async_copy(diff_hbm.at[:, y, :], df.at[rows], df_sem.at[y]).wait()
 
     pick = iota((CAP, levels), 1) - 3 * CAP == iota((CAP, levels), 0)
-    batch = n_all
+    for dst, sem in ((recv, v_recv), (mrecv, m_recv)):
+        part = dst.at[pl.ds(1, n_all - 1)]
+        pltpu.make_async_copy(part, part, sem.at[0]).wait()
     for k in range(n_all):
-        if k % batch == 0:
-            for copy in sends[max(2 * k - 2, 0) : 2 * (k + batch) - 2]:
-                copy.wait_recv()
         here = slice(k * CAP, (k + 1) * CAP)
         frac_y = (
             jnp.sum(jnp.where(pick, mrecv[k], 0.0), axis=1, keepdims=True) / SLOTS
@@ -405,8 +404,9 @@
     for j in range(1, HALF):
         finish_row(j)
         finish_row(lat - 1 - j)
-    for copy in sends:
-        copy.wait_send()
+    for src, sem in ((msg, v_send), (mmsg, m_send)):
+        part = src.at[pl.ds(1, n_all - 1)]
+        pltpu.make_async_copy(part, part, sem.at[0]).wait()
     halo(STEPS - 1)
     finish_row(0)
     finish_row(lat - 1)
@@ -417,13 +417,12 @@
 
     def store(y):
         return pltpu.make_async_copy(
-            rows_ref.at[pl.ds(y * lon, lon)], out_hbm.at[:, y, :], sem.at[y]
+            rows_ref.at[pl.ds(y * lon, lon)], out_hbm.at[:, y, :], sem.at[0]
         )
 
     for y in range(lat):
         store(y).start()
-    for y in range(lat):
-        store(y).wait()
+    pltpu.make_async_copy(rows_ref, rows_ref, sem.at[0]).wait()
 
 
 def solution(mesh):
@@ -473,7 +472,7 @@
                 pltpu.VMEM((2, 2, lon, levels), BF16),
                 pltpu.VMEM((STEPS, 2, lon, levels), BF16),
                 dma((5,)), dma((blocks,)), dma((lat,)), dma((lat,)),
-                dma((n_all,)), dma((n_all,)), dma((n_all,)), dma((n_all,)),
+                dma((1,)), dma((1,)), dma((1,)), dma((1,)),
                 dma((3,)), dma((3,)),
                 dma((STEPS, 2, blocks)), dma((STEPS, 2, blocks)),
                 dma((STEPS, 2)), dma((STEPS, 2)),
@@ -496,7 +495,7 @@
             out_shape=jax.ShapeDtypeStruct((lon, lat, levels), F32),
             in_specs=[vmem],
             out_specs=pl.BlockSpec(memory_space=pl.ANY),
-            scratch_shapes=[dma((lat,))],
+            scratch_shapes=[dma((1,))],
             compiler_params=pltpu.CompilerParams(vmem_limit_bytes=8 * 1024 * 1024),
             name="store",
         )(pltpu.with_memory_space_constraint(out, pltpu.VMEM))

time: 42.1 us -> 40.4 us (0.960)
  Pallas kernels: 41.9 us -> 40.3 us
    pallas_call x1, Pallas kernels: 39.4 us -> 38.3 us  [shards(): pl.pallas_call(functools.partial(kernel, n_gx, n_gy), out_shape=pltpu.VME...]
    pallas_call x1, Pallas kernels: 2.53 us -> 1.97 us  [shards(): pl.pallas_call(store_kernel, out_shape=jax.ShapeDtypeStruct((lon, lat, le...]
where the time goes in v3:
time: 40.4 us; the launch traced here: 40.3 us
  Pallas kernels  40.3 us (100%)
    pallas_call x1, Pallas kernels, shards(): pl.pallas_call(functools.partial(kernel, n_gx, n_gy), out_shape=pltpu.VME...  38.3 us
    pallas_call x1, Pallas kernels, shards(): pl.pallas_call(store_kernel, out_shape=jax.ShapeDtypeStruct((lon, lat, le...  1.97 us

profile of v3, /device:TPU:0, one launch (start us, length us, event | category | flops | bytes accessed | tf_op | source)
XLA Modules:
  0.0 40.3 jit_solution(2641824827149987977)
XLA Ops:
  0.0 38.3 %adjoint.1.rows_ref = f32[8192,128]{1,0:T(8,128)S(1)} custom-call(bf16[256,128]{1,0:T(8,128)(2,1)} %prof_hbm.1, s32[1,32]{1,0:T(1,128)} %counts_hbm.1, s32[1,256]{1,0:T(1,128)} %bitcast.2, s32[1,256]{1,0:T(1,128)} %bitcast.3, s32[2,256]{1,0:T(2,128)} %slot_hbm.1, f32[128,64,128]{2,1,0:T(8,128)} %state_hbm.1, f32[128,64,128]{2,1,0:T(8,128)} %diff_hbm.1, ...), custom_call_target="tpu_custom_call" | custom-call | tf_op jit(solution)/shard_map/adjoint/pallas_call | solution.py:440
  38.3 2.0 %store.1 = f32[128,64,128]{2,1,0:T(8,128)} custom-call(f32[8192,128]{1,0:T(8,128)S(1)} %adjoint.1.rows_ref), custom_call_target="tpu_custom_call" | custom-call | tf_op jit(solution)/shard_map/store/pallas_call | solution.py:493
